TPU v7x, 256 devices: a whole 4x4x8 slice. The times are simulated.
256 devices in a mesh: gx: 16 (over z, core), gy: 4 (over x), gz: 4 (over y).
Axes of the slice: x: 4, y: 4, z: 8, core: 2. Of those that a mesh axis runs over, the one named last changes fastest.
Arguments:
- block_values: bfloat16 [4, 64, 4, 6, 128, 128], P('gy', 'gx', 'gz'), as said below
- block_cols: int32 [4, 64, 4, 6], P('gy', 'gx', 'gz'), may hold values from 0 to 63, as said below
Outputs:
- purified: float32 [2048, 32768], P(('gx', 'gy'), 'gz')
Inputs may be any that keep to these rules, and one draw needn't show every extreme that they name: block_cols[a, s, b, :] holds 6 distinct tile columns of panel b at which tile row a * 64 + s of P is nonzero; every tile column of a panel is listed by exactly 6 tile rows of each slab; the pattern is symmetric: tile (i, j) is listed exactly when tile (j, i) is. `block_values`: P is symmetric: the tile listed at (i, j) is the transpose of the tile listed at (j, i), and diagonal tiles are symmetric.
All inputs are finite; a program needn't handle non-finite values.
Results may differ from a plain program's by a relative error of at most 0.0033.
Values may be sent and summed in bfloat16 or wider, within the bound.
A program may use at most 128 MiB of HBM per device.

v0:
```python
import jax
import jax.numpy as jnp
from jax import lax
from jax.sharding import PartitionSpec as P

WIN = 1


def picked_2(x, axis, root):
    return lax.dynamic_index_in_dim(lax.all_gather(x, axis), root, 0, keepdims=False)


def in_blocks(x, dim, length):
    lengths = x.shape
    tiles = x.reshape(*lengths[:dim], length, lengths[dim] // length, *lengths[dim + 1 :])
    return jnp.moveaxis(tiles, dim, 0)


def sent_and_summed(x, axis, dim):
    tiles = in_blocks(x, dim, lax.axis_size(axis))
    arrived = lax.all_to_all(tiles, axis, split_axis=0, concat_axis=0, tiled=True)
    return arrived.astype(jnp.float32).sum(axis=0)


def densify(left_tiles, left_columns, slab_tiles):
    onehot = (
        left_columns[:, :, None] == jnp.arange(slab_tiles, dtype=jnp.int32)[None, None, :]
    ).astype(jnp.bfloat16)
    densified = jnp.einsum("wkj,wkyx->wyjx", onehot, left_tiles, preferred_element_type=jnp.float32)
    tile_size = left_tiles.shape[2]
    return densified.astype(jnp.bfloat16).reshape(
        left_tiles.shape[0] * tile_size, slab_tiles, tile_size
    )


def product_one(left_panel, panel_tiles, panel_columns):
    summed = jnp.zeros(
        (left_panel.shape[0], panel_tiles.shape[0], panel_tiles.shape[2]), jnp.float32
    )
    for column_slot in range(panel_tiles.shape[1]):
        picked = jnp.take(left_panel, panel_columns[:, column_slot], axis=1)
        summed = summed + jnp.einsum(
            "rix,iyx->riy", picked, panel_tiles[:, column_slot], preferred_element_type=jnp.float32
        )
    return summed


def product_two(rounded, panel_tiles, panel_columns, panel_width):
    summed = jnp.zeros((rounded.shape[0], panel_width, panel_tiles.shape[3]), jnp.float32)
    for column_slot in range(panel_tiles.shape[1]):
        product = jnp.einsum(
            "rix,ixy->riy", rounded, panel_tiles[:, column_slot], preferred_element_type=jnp.float32
        )
        summed = summed.at[:, panel_columns[:, column_slot], :].add(product)
    return summed


def local(block_values, block_cols):
    tiles_here = block_values[0, :, 0]
    columns_here = block_cols[0, :, 0]
    tile_size = tiles_here.shape[2]
    slab_tiles = tiles_here.shape[0] * lax.axis_size("gx")
    left_tiles, left_columns = (
        picked_2(tiles_here[:WIN], "gy", 0),
        picked_2(columns_here[:WIN], "gy", 0),
    )
    left_panel = densify(left_tiles, left_columns, slab_tiles)
    height = left_panel.shape[0]
    on_diagonal = (lax.axis_index("gy") == lax.axis_index("gz")).astype(jnp.float32)
    panel_tiles, panel_columns = (
        lax.all_gather(tiles_here, "gx", axis=0, tiled=True),
        lax.all_gather(columns_here, "gx", axis=0, tiled=True),
    )
    partial_square = product_one(left_panel, panel_tiles, panel_columns)
    partial_square = partial_square.reshape(height, slab_tiles * tile_size)
    square = lax.psum(partial_square, "gz")
    square_low = square.astype(jnp.bfloat16).reshape(height, slab_tiles, tile_size)
    applied = product_two(square_low, panel_tiles, panel_columns, slab_tiles).reshape(
        height // lax.axis_size("gy") * lax.axis_size("gy"), slab_tiles * tile_size
    )
    return sent_and_summed(
        (3.0 * on_diagonal * square - 2.0 * applied).astype(jnp.bfloat16), "gy", 0
    )


def solution(mesh):
    in_specs = (P("gy", "gx", "gz", None, None, None), P("gy", "gx", "gz", None))
    out_specs = P(("gx", "gy"), "gz")
    return jax.shard_map(local, mesh=mesh, in_specs=in_specs, out_specs=out_specs, check_vma=False)
```

profile of v0, /device:TPU:32, one launch (start us, length us, event | category | flops | bytes accessed | tf_op | source)
XLA Modules:
  0.0 381.8 jit_solution(5912386459244780532)
XLA Ops:
  8.8 9.7 %all-gather = s32[4,1,1,6]{3,2,1,0:T(1,128)S(1)} all-gather(s32[1,1,1,6]{3,2,1,0:T(1,128)S(1)} %slice-done.4), channel_id=2, replica_groups=mesh['gx'=16,'gy'=4,'gz'=4] {'gy'}, dimensions={0}, use_global_device_ids=true | all-gather | bytes 120 | tf_op jit(solution)/shard_map/all_gather | solution.py:10
  18.5 13.3 %all-gather.1 = bf16[4,1,1,6,128,128]{5,4,3,2,1,0:T(8,128)(2,1)S(1)} all-gather(bf16[1,1,1,6,128,128]{5,4,3,2,1,0:T(8,128)(2,1)S(1)} %slice-done.3), channel_id=3, replica_groups=mesh['gx'=16,'gy'=4,'gz'=4] {'gy'}, dimensions={0}, use_global_device_ids=true | all-gather | bytes 983040 | tf_op jit(solution)/shard_map/all_gather | solution.py:10
  34.1 18.6 %all-gather.2 = s32[1,64,1,6]{3,2,0,1:T(1,128)S(1)} all-gather(s32[1,4,1,6]{3,2,0,1:T(1,128)S(1)} %bitcast.101), channel_id=4, replica_groups=mesh['gx'=16,'gy'=4,'gz'=4] {'gx'}, dimensions={1}, use_global_device_ids=true | all-gather | bytes 1632 | tf_op jit(solution)/shard_map/all_gather | solution.py:72
  66.1 19.6 %all-gather.6.cloned.1.call-done = bf16[1,64,1,6,128,128]{5,4,1,3,2,0:T(8,128)(2,1)} async-done(((bf16[1,4,1,6,128,128]{5,4,1,3,2,0:T(8,128)(2,1)}), bf16[1,64,1,6,128,128]{5,4,1,3,2,0:T(8,128)(2,1)}) %all-gather.6.cloned.1.call-update) | async-done | bytes 12582928 | tf_op jit(solution)/shard_map/all_gather | solution.py:71
  85.7 6.2 %fusion.10 = f32[64,128,128]{1,2,0:T(8,128)} fusion(bf16[64,128,128]{2,1,0:T(8,128)(2,1)} %gather_fusion, pred[64]{0:T(512)(128)(4,1)S(1)} %get-tuple-element.29, bf16[64,6,128,128]{3,2,0,1:T(8,128)(2,1)} %bitcast.84), kind=kOutput, calls=%fused_computation.31 | convolution fusion | flops 269484032 | bytes 8388672 | tf_op jit(solution)/shard_map/rix,iyx->riy/dot_general | solution.py:42
  91.8 6.0 %fusion.2 = f32[64,128,128]{1,2,0:T(8,128)} fusion(bf16[64,128,128]{2,1,0:T(8,128)(2,1)} %gather_fusion.4, pred[64]{0:T(512)(128)(4,1)S(1)} %get-tuple-element.25, bf16[64,6,128,128]{3,2,0,1:T(8,128)(2,1)} %bitcast.85), kind=kOutput, calls=%fused_computation.23 | convolution fusion | flops 269484032 | bytes 8388672 | tf_op jit(solution)/shard_map/rix,iyx->riy/dot_general | solution.py:42
  97.8 3.6 fusion.4
  101.5 3.6 fusion.6
  105.1 3.6 fusion.8
  108.7 10.1 %add_add_fusion = f32[64,128,128]{1,2,0:T(8,128)} fusion(f32[64,128,128]{1,2,0:T(8,128)} %fusion.2, f32[64,128,128]{1,2,0:T(8,128)} %fusion.4, f32[64,128,128]{1,2,0:T(8,128)} %fusion.6, f32[64,128,128]{1,2,0:T(8,128)} %fusion.10, f32[64,128,128]{1,2,0:T(8,128)} %fusion.8, bf16[64,128,128]{2,1,0:T(8,128)(2,1)S(1)} %copy-done.4, ...), kind=kOutput, calls=%fused_computation.15 | convolution fusion | flops 274726912 | bytes 29360640 | tf_op jit(solution)/shard_map/rix,iyx->riy/dot_general | solution.py:42
  118.8 98.5 %all-reduce.2.cloned.1.call-done = f32[128,8192]{0,1:T(8,128)} async-done(((f32[128,8192]{0,1:T(8,128)}), f32[128,8192]{0,1:T(8,128)}) %all-reduce.2.cloned.1.call-update) | async-done | bytes 4194320 | tf_op jit(solution)/shard_map/psum | solution.py:76
  219.9 4.6 %fusion.24 = f32[64,128,128]{2,1,0:T(8,128)} fusion(bf16[128,64,128]{0,2,1:T(8,128)(2,1)S(1)} %bitcast.78, bf16[64,6,128,128]{3,2,0,1:T(8,128)(2,1)} %bitcast.86), kind=kOutput, calls=%fused_computation.47 | convolution fusion | flops 268435456 | bytes 8388608 | tf_op jit(solution)/shard_map/rix,ixy->riy/dot_general | solution.py:51
  224.5 4.6 %fusion.25 = f32[64,128,128]{2,1,0:T(8,128)} fusion(bf16[128,64,128]{0,2,1:T(8,128)(2,1)S(1)} %bitcast.79, bf16[64,6,128,128]{3,2,0,1:T(8,128)(2,1)} %bitcast.87), kind=kOutput, calls=%fused_computation.48 | convolution fusion | flops 268435456 | bytes 8388608 | tf_op jit(solution)/shard_map/rix,ixy->riy/dot_general | solution.py:51
  242.8 13.7 %scatter_fusion = f32[128,64,128]{2,0,1:T(8,128)} fusion(f32[128,64,128]{2,0,1:T(8,128)} %broadcast_in_dim.11, s32[64]{0:T(128)S(1)} %get-tuple-element.7, f32[64,128,128]{2,1,0:T(8,128)} %fusion.24), kind=kCustom, calls=%fused_computation.6 | custom fusion | flops 1048576 | bytes 12583168 | tf_op jit(solution)/shard_map/scatter-add | solution.py:54
  256.5 13.7 %scatter_fusion.1 = f32[128,64,128]{2,0,1:T(8,128)} fusion(f32[128,64,128]{2,0,1:T(8,128)} %scatter_fusion, s32[64]{0:T(128)S(1)} %get-tuple-element.8, f32[64,128,128]{2,1,0:T(8,128)} %fusion.25), kind=kCustom, calls=%fused_computation.7 | custom fusion | flops 1048576 | bytes 12583168 | tf_op jit(solution)/shard_map/scatter-add | solution.py:54
  270.2 13.7 %scatter_fusion.2 = f32[128,64,128]{2,0,1:T(8,128)} fusion(f32[128,64,128]{2,0,1:T(8,128)} %scatter_fusion.1, s32[64]{0:T(128)S(1)} %get-tuple-element.9, f32[64,128,128]{2,1,0:T(8,128)} %fusion.26), kind=kCustom, calls=%fused_computation.8 | custom fusion | flops 1048576 | bytes 12583168 | tf_op jit(solution)/shard_map/scatter-add | solution.py:54
  283.9 13.6 %scatter_fusion.3 = f32[128,64,128]{2,0,1:T(8,128)} fusion(f32[128,64,128]{2,0,1:T(8,128)} %scatter_fusion.2, s32[64]{0:T(128)S(1)} %get-tuple-element.10, f32[64,128,128]{2,1,0:T(8,128)} %fusion.27), kind=kCustom, calls=%fused_computation.9 | custom fusion | flops 1048576 | bytes 12583168 | tf_op jit(solution)/shard_map/scatter-add | solution.py:54
  297.5 13.7 %scatter_fusion.4 = f32[128,64,128]{2,0,1:T(8,128)} fusion(f32[128,64,128]{2,0,1:T(8,128)} %scatter_fusion.3, s32[64]{0:T(128)S(1)} %get-tuple-element.11, f32[64,128,128]{2,1,0:T(8,128)} %fusion.28), kind=kCustom, calls=%fused_computation.10 | custom fusion | flops 1048576 | bytes 12583168 | tf_op jit(solution)/shard_map/scatter-add | solution.py:54
  311.1 13.6 %scatter_fusion.5 = f32[128,64,128]{2,0,1:T(8,128)} fusion(f32[128,64,128]{2,0,1:T(8,128)} %scatter_fusion.4, s32[64]{0:T(128)S(1)} %get-tuple-element.6, f32[64,128,128]{2,1,0:T(8,128)} %fusion.29), kind=kCustom, calls=%fused_computation.11 | custom fusion | flops 1048576 | bytes 12583168 | tf_op jit(solution)/shard_map/scatter-add | solution.py:54
  324.8 4.7 %broadcast_multiply_fusion = f32[128,64,128]{2,0,1:T(8,128)} fusion(f32[128,64,128]{2,0,1:T(8,128)} %scatter_fusion.5), kind=kLoop, calls=%fused_computation.39 | loop fusion | flops 1048576 | bytes 8388608 | tf_op jit(solution)/shard_map/mul | solution.py:82
  329.5 5.6 %copy.42 = f32[128,64,128]{0,2,1:T(8,128)} copy(f32[128,64,128]{2,0,1:T(8,128)} %broadcast_multiply_fusion) | data formatting | bytes 8388608 | tf_op jit(solution)/shard_map/mul | solution.py:82
  335.1 5.2 %fusion = bf16[128,8192]{0,1:T(8,128)(2,1)} fusion(f32[128,64,128]{0,2,1:T(8,128)} %copy.42, f32[128,8192]{0,1:T(8,128)} %all-reduce.2.cloned.1.call-done, f32[]{:T(128)S(6)} %mul_shard_map.3), kind=kLoop, calls=%fused_computation.13 | loop fusion | flops 3145728 | bytes 10485764 | tf_op jit(solution)/shard_map/convert_element_type | solution.py:82
  340.3 2.9 copy.43
  343.3 30.4 %all_to_all.5 = bf16[4,32,8192]{2,1,0:T(8,128)(2,1)S(1)} all-to-all(bf16[4,32,8192]{2,1,0:T(8,128)(2,1)S(1)} %bitcast.99), channel_id=1, replica_groups=mesh['gx'=16,'gy'=4,'gz'=4] {'gy'}, dimensions={0} | all-to-all | bytes 4194304 | tf_op jit(solution)/shard_map/all_to_all | solution.py:21
  (58 shorter events, 35.4 us)
Async XLA Ops:
  6.5 12.0 %slice-start.3 = ((bf16[1,4,1,6,128,128]{5,4,3,2,1,0:T(8,128)(2,1)}), bf16[1,1,1,6,128,128]{5,4,3,2,1,0:T(8,128)(2,1)S(1)}, s32[]{:S(2)}) async-start(bf16[1,4,1,6,128,128]{5,4,3,2,1,0:T(8,128)(2,1)} %param.4), calls=%async_computation.6 | async-start | bytes 393216 | tf_op jit(solution)/shard_map/slice | solution.py:64
  6.5 2.2 slice-start.4
  6.5 79.1 %all-gather.6.cloned.1.call-start = ((), (), s32[]{:S(2)}) async-start(), calls=%async_computation.2 | async-start | bytes 13369344 | tf_op jit(solution)/shard_map/all_gather | solution.py:71
  8.7 208.6 %all-reduce.2.cloned.1.call-start = ((), (), s32[]{:S(2)}) async-start(), calls=%async_computation.1 | async-start | bytes 8388608 | tf_op jit(solution)/shard_map/psum | solution.py:76
  32.7 1.4 copy-start.5
  85.7 12.2 %copy-start = (bf16[1,64,1,6,128,128]{5,4,1,3,2,0:T(8,128)(2,1)S(1)}, bf16[1,64,1,6,128,128]{5,4,1,3,2,0:T(8,128)(2,1)}, u32[]{:S(2)}) copy-start(bf16[1,64,1,6,128,128]{5,4,1,3,2,0:T(8,128)(2,1)} %all-gather.6.cloned.1.call-done) | copy-start | bytes 37748740
  91.8 6.0 %copy-start.1 = (bf16[64,128,128]{2,1,0:T(8,128)(2,1)S(1)}, bf16[64,128,128]{2,1,0:T(8,128)(2,1)}, u32[]{:S(2)}) copy-start(bf16[64,128,128]{2,1,0:T(8,128)(2,1)} %gather_fusion.3) | copy-start | bytes 6291460
  97.8 3.6 copy-start.2
  101.5 3.6 copy-start.3
  105.1 3.6 copy-start.4
  217.4 11.7 %slice-start = ((s8[12582912]{0:T(1024)(128)(4,1)}), s8[4194304]{0:T(1024)(128)(4,1)S(1)}, s32[]{:S(2)}) async-start(s8[12582912]{0:T(1024)(128)(4,1)} %bitcast.92), calls=%async_computation.3 | async-start | bytes 8388608
  219.9 9.2 %slice-start.1 = ((s8[12582912]{0:T(1024)(128)(4,1)}), s8[4194304]{0:T(1024)(128)(4,1)S(1)}, s32[]{:S(2)}) async-start(s8[12582912]{0:T(1024)(128)(4,1)} %bitcast.92), calls=%async_computation.4 | async-start | bytes 8388608
  224.5 4.6 %slice-start.2 = ((s8[12582912]{0:T(1024)(128)(4,1)}), s8[4194304]{0:T(1024)(128)(4,1)S(1)}, s32[]{:S(2)}) async-start(s8[12582912]{0:T(1024)(128)(4,1)} %bitcast.92), calls=%async_computation.5 | async-start | bytes 8388608
Sparse Core Ops, SparseCore 0:
  9.2 76.4 all-gather.5
  118.9 98.3 all-reduce.1
where the time goes:
time: 383 us; the launch traced here: 382 us
  waiting for transfers between devices  118 us (31%)
  other arithmetic  96.3 us (25%)
  blocking collectives  72 us (19%)
  matrix products  54.3 us (14%)
  local copies, waits for them, and re-layouts  27.4 us (7%)
  between operations  13.5 us (4%)
    psum x1, waiting for transfers between devices, local(): square = lax.psum(partial_square, 'gz')  98.5 us
    scatter-add x6, other arithmetic, product_two(): summed = summed.at[:, panel_columns[:, column_slot], :].add(product)  82 us
    dot_general x6, matrix products, product_one(): jnp.einsum('rix,iyx->riy', picked, panel_tiles[:, column_slot], preferred...  33.1 us
    all_to_all x1, blocking collectives, sent_and_summed(): lax.all_to_all(tiles, axis, split_axis=0, concat_axis=0, tiled=True)  30.4 us
    all_gather x2, blocking collectives, picked_2(): lax.all_gather(x, axis)  23 us
    dot_general x6, matrix products, product_two(): jnp.einsum('rix,ixy->riy', rounded, panel_tiles[:, column_slot], preferre...  20.4 us
    all_gather x1, waiting for transfers between devices, local(): lax.all_gather(tiles_here, 'gx', axis=0, tiled=True)  19.6 us
    all_gather x1, blocking collectives, local(): lax.all_gather(columns_here, 'gx', axis=0, tiled=True)  18.6 us
  transfers between devices with their start and end apart: 2, of which 2 were waited for; matrix products, arithmetic and copies ran while one was open for 4% of the time, Pallas kernels for 0%

commit v1 on v0

--- a/solution.py
+++ b/solution.py
@@ -73,7 +73,7 @@
     )
     partial_square = product_one(left_panel, panel_tiles, panel_columns)
     partial_square = partial_square.reshape(height, slab_tiles * tile_size)
-    square = lax.psum(partial_square, "gz")
+    square = jnp.sum(lax.all_gather(partial_square, "gz"), axis=0)
     square_low = square.astype(jnp.bfloat16).reshape(height, slab_tiles, tile_size)
     applied = product_two(square_low, panel_tiles, panel_columns, slab_tiles).reshape(
         height // lax.axis_size("gy") * lax.axis_size("gy"), slab_tiles * tile_size

time: 383 us -> 470 us (1.23)
  waiting for transfers between devices: 118 us -> 175 us
  local copies, waits for them, and re-layouts: 27.4 us -> 46.7 us
  other arithmetic: 96.3 us -> 106 us
    all_gather x0 -> x1, waiting for transfers between devices: none -> 157 us  [local(): square = jnp.sum(lax.all_gather(partial_square, 'gz'), axis=0)]
    psum x1 -> x0, waiting for transfers between devices: 98.5 us -> none  [local(): square = lax.psum(partial_square, 'gz')]
    reduce_sum x0 -> x1, other arithmetic: none -> 9.45 us  [local(): square = jnp.sum(lax.all_gather(partial_square, 'gz'), axis=0)]
    mul x0 -> x1, local copies, waits for them, and re-layouts: none -> 5.65 us  [local(): 3.0 * on_diagonal * square - 2.0 * applied]
    another operation x0 -> x1, local copies, waits for them, and re-layouts: none -> 5.6 us  [local(): square = jnp.sum(lax.all_gather(partial_square, 'gz'), axis=0)]
    unnamed x19 -> x20, local copies, waits for them, and re-layouts: 2.19 us -> 7.73 us
where the time goes in v1:
time: 470 us; the launch traced here: 468 us
  waiting for transfers between devices  175 us (37%)
  other arithmetic  106 us (23%)
  blocking collectives  71.8 us (15%)
  matrix products  54.4 us (12%)
  local copies, waits for them, and re-layouts  46.7 us (10%)
  between operations  13.5 us (3%)
    all_gather x1, waiting for transfers between devices, local(): square = jnp.sum(lax.all_gather(partial_square, 'gz'), axis=0)  157 us
    scatter-add x6, other arithmetic, product_two(): summed = summed.at[:, panel_columns[:, column_slot], :].add(product)  82.2 us
    dot_general x6, matrix products, product_one(): jnp.einsum('rix,iyx->riy', picked, panel_tiles[:, column_slot], preferred...  33.3 us
    all_to_all x1, blocking collectives, sent_and_summed(): lax.all_to_all(tiles, axis, split_axis=0, concat_axis=0, tiled=True)  30.2 us
    all_gather x2, blocking collectives, picked_2(): lax.all_gather(x, axis)  23 us
    dot_general x6, matrix products, product_two(): jnp.einsum('rix,ixy->riy', rounded, panel_tiles[:, column_slot], preferre...  20.3 us
    all_gather x1, blocking collectives, local(): lax.all_gather(columns_here, 'gx', axis=0, tiled=True)  18.6 us
    all_gather x1, waiting for transfers between devices, local(): lax.all_gather(tiles_here, 'gx', axis=0, tiled=True)  18 us
  transfers between devices with their start and end apart: 2, of which 2 were waited for; matrix products, arithmetic and copies ran while one was open for 4% of the time, Pallas kernels for 0%

profile of v1, /device:TPU:32, one launch (start us, length us, event | category | flops | bytes accessed | tf_op | source)
XLA Modules:
  0.0 467.9 jit_solution(3969880518924371694)
XLA Ops:
  9.4 9.7 %all-gather = s32[4,1,1,6]{3,2,1,0:T(1,128)S(1)} all-gather(s32[1,1,1,6]{3,2,1,0:T(1,128)S(1)} %slice.58), channel_id=2, replica_groups=mesh['gx'=16,'gy'=4,'gz'=4] {'gy'}, dimensions={0}, use_global_device_ids=true | all-gather | bytes 120 | tf_op jit(solution)/shard_map/all_gather | solution.py:10
  20.0 13.3 %all-gather.1 = bf16[4,1,1,6,128,128]{5,4,3,2,1,0:T(8,128)(2,1)S(1)} all-gather(bf16[1,1,1,6,128,128]{5,4,3,2,1,0:T(8,128)(2,1)S(1)} %slice.59), channel_id=3, replica_groups=mesh['gx'=16,'gy'=4,'gz'=4] {'gy'}, dimensions={0}, use_global_device_ids=true | all-gather | bytes 983040 | tf_op jit(solution)/shard_map/all_gather | solution.py:10
  35.6 18.6 %all-gather.2 = s32[1,64,1,6]{3,2,0,1:T(1,128)S(1)} all-gather(s32[1,4,1,6]{3,2,0,1:T(1,128)S(1)} %bitcast.97), channel_id=4, replica_groups=mesh['gx'=16,'gy'=4,'gz'=4] {'gx'}, dimensions={1}, use_global_device_ids=true | all-gather | bytes 1632 | tf_op jit(solution)/shard_map/all_gather | solution.py:72
  67.6 18.0 %all-gather.9.cloned.1.call-done = bf16[1,64,1,6,128,128]{5,4,1,3,2,0:T(8,128)(2,1)} async-done(((bf16[1,4,1,6,128,128]{5,4,1,3,2,0:T(8,128)(2,1)}), bf16[1,64,1,6,128,128]{5,4,1,3,2,0:T(8,128)(2,1)}) %all-gather.9.cloned.1.call-update) | async-done | bytes 12582928 | tf_op jit(solution)/shard_map/all_gather | solution.py:71
  85.7 6.2 %fusion.3 = f32[64,128,128]{1,2,0:T(8,128)} fusion(bf16[64,128,128]{2,1,0:T(8,128)(2,1)} %gather_fusion.3, pred[64]{0:T(512)(128)(4,1)S(1)} %get-tuple-element.28, bf16[64,6,128,128]{3,2,0,1:T(8,128)(2,1)} %bitcast.80), kind=kOutput, calls=%fused_computation.24 | convolution fusion | flops 269484032 | bytes 8388672 | tf_op jit(solution)/shard_map/rix,iyx->riy/dot_general | solution.py:42
  91.8 6.0 %fusion.5 = f32[64,128,128]{1,2,0:T(8,128)} fusion(bf16[64,128,128]{2,1,0:T(8,128)(2,1)} %gather_fusion.2, pred[64]{0:T(512)(128)(4,1)S(1)} %get-tuple-element.29, bf16[64,6,128,128]{3,2,0,1:T(8,128)(2,1)} %bitcast.81), kind=kOutput, calls=%fused_computation.26 | convolution fusion | flops 269484032 | bytes 8388672 | tf_op jit(solution)/shard_map/rix,iyx->riy/dot_general | solution.py:42
  108.9 10.2 %add_add_fusion = f32[64,128,128]{1,2,0:T(8,128)} fusion(f32[64,128,128]{1,2,0:T(8,128)} %fusion.1, f32[64,128,128]{1,2,0:T(8,128)} %fusion.3, f32[64,128,128]{1,2,0:T(8,128)} %fusion.5, f32[64,128,128]{1,2,0:T(8,128)} %fusion.9, f32[64,128,128]{1,2,0:T(8,128)} %fusion.7, bf16[64,128,128]{2,1,0:T(8,128)(2,1)S(1)} %copy-done.4, ...), kind=kOutput, calls=%fused_computation.14 | convolution fusion | flops 274726912 | bytes 29360640 | tf_op jit(solution)/shard_map/rix,iyx->riy/dot_general | solution.py:42
  119.0 5.6 %copy.52 = f32[1,128,8192]{2,1,0:T(8,128)} copy(f32[1,128,8192]{1,2,0:T(8,128)} %bitcast.95) | data formatting | bytes 8388608 | tf_op jit(solution)/shard_map/all_gather;reshape | solution.py:76
  124.7 157.2 %all-gather.7.cloned.1.call-done = f32[4,128,8192]{2,1,0:T(8,128)} async-done(((f32[1,128,8192]{2,1,0:T(8,128)}), f32[4,128,8192]{2,1,0:T(8,128)}) %all-gather.7.cloned.1.call-update) | async-done | bytes 16777232 | tf_op jit(solution)/shard_map/all_gather | solution.py:76
  281.9 9.5 %reduce_sum.18 = f32[128,8192]{1,0:T(8,128)} reduce(f32[4,128,8192]{2,1,0:T(8,128)} %all-gather.7.cloned.1.call-done, f32[]{:T(128)} %constant.20.clone.1), dimensions={0}, to_apply=%region_0.2 | reduce | flops 3145728 | bytes 20971524 | tf_op jit(solution)/shard_map/reduce_sum | solution.py:76
  291.3 5.6 %copy.68 = f32[128,8192]{0,1:T(8,128)} copy(f32[128,8192]{1,0:T(8,128)} %reduce_sum.18) | data formatting | bytes 8388608
  296.9 6.3 %fusion.50 = (bf16[128,8192]{0,1:T(8,128)(2,1)S(1)}, f32[128,8192]{0,1:T(8,128)}) fusion(f32[128,8192]{0,1:T(8,128)} %copy.68, f32[]{:T(128)S(6)} %mul_shard_map.3), kind=kLoop, calls=%fused_computation.106 | loop fusion | flops 2097152 | bytes 10485764 | tf_op jit(solution)/shard_map/convert_element_type | solution.py:77
  303.2 4.6 fusion.23
  307.8 4.4 fusion.24
  326.0 13.7 %scatter_fusion = f32[128,64,128]{2,0,1:T(8,128)} fusion(f32[128,64,128]{2,0,1:T(8,128)} %broadcast_in_dim.11, s32[64]{0:T(128)S(1)} %get-tuple-element.7, f32[64,128,128]{2,1,0:T(8,128)} %fusion.23), kind=kCustom, calls=%fused_computation.6 | custom fusion | flops 1048576 | bytes 12583168 | tf_op jit(solution)/shard_map/scatter-add | solution.py:54
  339.7 13.7 %scatter_fusion.1 = f32[128,64,128]{2,0,1:T(8,128)} fusion(f32[128,64,128]{2,0,1:T(8,128)} %scatter_fusion, s32[64]{0:T(128)S(1)} %get-tuple-element.8, f32[64,128,128]{2,1,0:T(8,128)} %fusion.24), kind=kCustom, calls=%fused_computation.7 | custom fusion | flops 1048576 | bytes 12583168 | tf_op jit(solution)/shard_map/scatter-add | solution.py:54
  353.3 13.7 %scatter_fusion.2 = f32[128,64,128]{2,0,1:T(8,128)} fusion(f32[128,64,128]{2,0,1:T(8,128)} %scatter_fusion.1, s32[64]{0:T(128)S(1)} %get-tuple-element.9, f32[64,128,128]{2,1,0:T(8,128)} %fusion.25), kind=kCustom, calls=%fused_computation.8 | custom fusion | flops 1048576 | bytes 12583168 | tf_op jit(solution)/shard_map/scatter-add | solution.py:54
  367.0 13.9 %scatter_fusion.3 = f32[128,64,128]{2,0,1:T(8,128)} fusion(f32[128,64,128]{2,0,1:T(8,128)} %scatter_fusion.2, s32[64]{0:T(128)S(1)} %get-tuple-element.10, f32[64,128,128]{2,1,0:T(8,128)} %fusion.26), kind=kCustom, calls=%fused_computation.9 | custom fusion | flops 1048576 | bytes 12583168 | tf_op jit(solution)/shard_map/scatter-add | solution.py:54
  380.9 13.7 %scatter_fusion.4 = f32[128,64,128]{2,0,1:T(8,128)} fusion(f32[128,64,128]{2,0,1:T(8,128)} %scatter_fusion.3, s32[64]{0:T(128)S(1)} %get-tuple-element.11, f32[64,128,128]{2,1,0:T(8,128)} %fusion.27), kind=kCustom, calls=%fused_computation.10 | custom fusion | flops 1048576 | bytes 12583168 | tf_op jit(solution)/shard_map/scatter-add | solution.py:54
  394.6 13.6 %scatter_fusion.5 = f32[128,64,128]{2,0,1:T(8,128)} fusion(f32[128,64,128]{2,0,1:T(8,128)} %scatter_fusion.4, s32[64]{0:T(128)S(1)} %get-tuple-element.6, f32[64,128,128]{2,1,0:T(8,128)} %fusion.28), kind=kCustom, calls=%fused_computation.11 | custom fusion | flops 1048576 | bytes 12583168 | tf_op jit(solution)/shard_map/scatter-add | solution.py:54
  410.7 4.4 copy.61
  415.1 4.9 %mul.25 = f32[4,32,8192]{2,1,0:T(8,128)} reshape(f32[128,64,128]{2,1,0:T(8,128)} %copy.61) | data formatting | bytes 8388608 | tf_op jit(solution)/shard_map/mul | solution.py:82
  420.1 5.6 %copy.54 = f32[128,8192]{1,0:T(8,128)} copy(f32[128,8192]{0,1:T(8,128)} %get-tuple-element.19) | data formatting | bytes 8388608 | tf_op jit(solution)/shard_map/mul | solution.py:82
  429.6 30.2 %all_to_all.5 = bf16[4,32,8192]{2,1,0:T(8,128)(2,1)S(1)} all-to-all(bf16[4,32,8192]{2,1,0:T(8,128)(2,1)S(1)} %subtract_convert_fusion), channel_id=1, replica_groups=mesh['gx'=16,'gy'=4,'gz'=4] {'gy'}, dimensions={0} | all-to-all | bytes 4194304 | tf_op jit(solution)/shard_map/all_to_all | solution.py:21
  (60 shorter events, 51.9 us)
Async XLA Ops:
  6.5 79.1 %all-gather.9.cloned.1.call-start = ((), (), s32[]{:S(2)}) async-start(), calls=%async_computation.2 | async-start | bytes 13369344 | tf_op jit(solution)/shard_map/all_gather | solution.py:71
  8.6 26.9 %copy-start.5 = (s32[1,4,1,6]{3,2,1,0:T(1,128)S(1)}, s32[1,4,1,6]{3,2,1,0:T(1,128)}, u32[]{:S(2)}) copy-start(s32[1,4,1,6]{3,2,1,0:T(1,128)} %param.5) | copy-start | bytes 292
  8.7 273.2 %all-gather.7.cloned.1.call-start = ((), (), s32[]{:S(2)}) async-start(), calls=%async_computation.1 | async-start | bytes 20971520 | tf_op jit(solution)/shard_map/all_gather | solution.py:76
  85.7 12.2 %copy-start = (bf16[1,64,1,6,128,128]{5,4,1,3,2,0:T(8,128)(2,1)S(1)}, bf16[1,64,1,6,128,128]{5,4,1,3,2,0:T(8,128)(2,1)}, u32[]{:S(2)}) copy-start(bf16[1,64,1,6,128,128]{5,4,1,3,2,0:T(8,128)(2,1)} %all-gather.9.cloned.1.call-done) | copy-start | bytes 37748740
  91.8 6.0 %copy-start.1 = (bf16[64,128,128]{2,1,0:T(8,128)(2,1)S(1)}, bf16[64,128,128]{2,1,0:T(8,128)(2,1)}, u32[]{:S(2)}) copy-start(bf16[64,128,128]{2,1,0:T(8,128)(2,1)} %gather_fusion.1) | copy-start | bytes 6291460
  97.8 3.7 copy-start.2
  101.5 3.6 copy-start.3
  105.1 3.7 copy-start.4
  296.9 15.3 %slice-start = ((s8[12582912]{0:T(1024)(128)(4,1)}), s8[4194304]{0:T(1024)(128)(4,1)S(1)}, s32[]{:S(2)}) async-start(s8[12582912]{0:T(1024)(128)(4,1)} %bitcast.88), calls=%async_computation.3 | async-start | bytes 8388608
  296.9 15.3 %slice-start.1 = ((s8[12582912]{0:T(1024)(128)(4,1)}), s8[4194304]{0:T(1024)(128)(4,1)S(1)}, s32[]{:S(2)}) async-start(s8[12582912]{0:T(1024)(128)(4,1)} %bitcast.88), calls=%async_computation.4 | async-start | bytes 8388608
  303.2 9.0 %slice-start.2 = ((s8[12582912]{0:T(1024)(128)(4,1)}), s8[4194304]{0:T(1024)(128)(4,1)S(1)}, s32[]{:S(2)}) async-start(s8[12582912]{0:T(1024)(128)(4,1)} %bitcast.88), calls=%async_computation.5 | async-start | bytes 8388608
Sparse Core Ops, SparseCore 0:
  9.2 76.4 all-gather.8
  124.8 157.0 all-gather.6
